TPU v7x, 32 devices: a whole 2x2x4 slice. The times are simulated.
32 devices in a mesh: groups: 2 (over x), kv: 16 (over z, y, core).
Axes of the slice: x: 2, y: 2, z: 4, core: 2. Of those that a mesh axis runs over, the one named last changes fastest.
Arguments:
- queries: bfloat16 [80, 18432], P('groups', 'kv'), parts along dimension 0, may hold values from -240 to 240
- latent_cache: bfloat16 [80, 2048, 576], P('groups', 'kv'), parts along dimension 0, may hold values from -6 to 6
- context_lengths: int32 [80], P('groups'), parts along dimension 0, may hold values from 128 to 2048, as said below
- value_up: bfloat16 [16384, 128], P('kv'), may hold values from -0.25 to 0.25
- out_proj: bfloat16 [4096, 7168], P('kv'), may hold values from -0.09375 to 0.09375
- residual: bfloat16 [80, 7168], P('groups', 'kv'), parts along dimension 0, may hold values from -0.75 to 0.75
- norm_gain: bfloat16 [7168], P('kv'), may hold values from 0.5 to 1.5
- expert_ids: int32 [80, 8], P('groups'), parts along dimension 0, may hold values from 0 to 255, all different within a row; in each aligned block of 40 rows (0 to 39, 40 to 79, ...) at most 2 rows name the same one
- gate_weights: float32 [80, 8], P('groups'), parts along dimension 0, may hold values from 0.05 to 0.5
Outputs:
- dispatched: bfloat16 [512, 2, 7168], P(('groups', 'kv')), parts along dimension 0
- slot_scale: float32 [512, 2], P(('groups', 'kv')), parts along dimension 0
- slot_gate: float32 [512, 2], P(('groups', 'kv')), parts along dimension 0
There are 2 independent parts, one for each index of `groups`. A program takes and returns all parts, laid end to end along the dimension named above; an argument that names none is the same for every part. Nothing has to cross between parts.
Inputs may be any that keep to these rules, and one draw needn't show every extreme that they name: `context_lengths`: multiples of 128; some sequence is 2048 long. `expert_ids`: each token names 8 different experts; no expert is named by more than 2 tokens, a bound that some block reaches.
All inputs are finite; a program needn't handle non-finite values. Where the computation divides by a largest or mean magnitude, that divisor is 1e-20 or more.
Results may differ from a plain program's by a relative error of at most 0.0069.
Values may be sent and summed in bfloat16 or wider, within the bound.
A program may use at most 64 MiB of HBM per device.

v0:
```python
import jax
import jax.numpy as jnp
from jax import lax
from jax.sharding import PartitionSpec as P

H = 32
LAT = 512
ROPE = 64
VD = 128
D = 7168
EXPERTS = 256
TOPK = 8
CAP = 2
score_scale = 192.0 ** (-0.5)
masked_score = -1e30
small_eps = 1e-06


def from_partner(value, axis, bit):
    mask = 2**bit
    pairs = [(source, source ^ mask) for source in range(lax.axis_size(axis))]
    return lax.ppermute(value, axis, pairs)


def slot_targets(expert_ids):
    flat_ids = expert_ids.reshape(-1)
    order_index = jnp.arange(flat_ids.shape[0], dtype=jnp.int32)
    same_before = (flat_ids[:, None] == flat_ids[None, :]) & (
        order_index[None, :] < order_index[:, None]
    )
    rank_within = jnp.sum(same_before.astype(jnp.int32), axis=1)
    return flat_ids * CAP + rank_within


def slot_match(targets, first_slot, slot_count):
    slot_index = first_slot + jnp.arange(slot_count, dtype=jnp.int32)
    return (slot_index[:, None] == targets[None, :]).astype(jnp.float32)


def token_picker(matches, seq_count):
    return jnp.sum(matches.reshape(matches.shape[0], seq_count, TOPK), axis=2)


def per_device(
    queries,
    latent_cache,
    context_lengths,
    value_up,
    out_proj,
    residual,
    norm_gain,
    expert_ids,
    gate_weights,
):
    kv_count = lax.axis_size("kv")
    shard_index = lax.axis_index("kv")
    seq_count = queries.shape[0]
    query_rows = lax.all_gather(queries, "kv", axis=1, tiled=True).reshape(seq_count, H, LAT + ROPE)
    ctx_local = latent_cache.shape[1]
    scores = (
        jnp.einsum("shq,scq->shc", query_rows, latent_cache, preferred_element_type=jnp.float32)
        * score_scale
    )
    position = shard_index * ctx_local + jnp.arange(ctx_local, dtype=jnp.int32)
    valid_mask = (position[None, :] < context_lengths[:, None])[:, None, :]
    scores = jnp.where(valid_mask, scores, masked_score)
    local_max = jnp.max(scores, axis=2)
    weights = jnp.where(valid_mask, jnp.exp(scores - local_max[:, :, None]), 0.0)
    local_total = jnp.sum(weights, axis=2)
    local_out = jnp.einsum(
        "shc,scl->shl",
        weights.astype(jnp.bfloat16),
        latent_cache[:, :, :LAT],
        preferred_element_type=jnp.float32,
    )
    out_rows = out_proj.shape[0]
    col_count = H * LAT // kv_count
    segment = min(col_count, LAT)
    head_count = col_count // segment
    head_start = shard_index * col_count // LAT
    global_max = lax.pmax(local_max, "kv")
    scaling = jnp.exp(local_max - global_max)
    weight_total = lax.psum(local_total * scaling, "kv")
    scaled = (local_out * scaling[:, :, None]).reshape(seq_count, H * LAT)
    merged_sum = lax.psum_scatter(scaled, "kv", scatter_dimension=1, tiled=True).reshape(
        seq_count, head_count, segment
    )
    own_total = lax.dynamic_slice_in_dim(weight_total, head_start, head_count, 1)
    merged = merged_sum / own_total[:, :, None]
    projector = value_up.reshape(head_count, segment, VD).astype(jnp.float32)
    value_part = jnp.einsum("shl,hlv->shv", merged, projector, precision=lax.Precision.HIGHEST)
    holders = kv_count // H if kv_count > H else 1
    for bit in range(holders.bit_length() - 1):
        value_part = value_part + from_partner(value_part, "kv", bit)
    value_rows = value_part.astype(jnp.bfloat16).reshape(seq_count, head_count * VD)
    if holders > 1:
        value_rows = lax.dynamic_slice_in_dim(
            value_rows, shard_index % holders * out_rows, out_rows, 1
        )
    partial_out = jnp.dot(value_rows, out_proj, preferred_element_type=jnp.float32)
    experts_local = EXPERTS // kv_count
    slot_count = experts_local * CAP
    targets = slot_targets(expert_ids)
    own_match = slot_match(targets, shard_index * slot_count, slot_count)
    own_pick = token_picker(own_match, seq_count)
    slot_gate = jnp.dot(own_match, gate_weights.reshape(-1), precision=lax.Precision.HIGHEST)
    attn_rows = lax.psum(partial_out, "kv")
    resid_rows, gain_cols = (
        lax.all_gather(residual, "kv", axis=1, tiled=True),
        lax.all_gather(norm_gain, "kv", axis=0, tiled=True),
    )
    summed = attn_rows + resid_rows.astype(jnp.float32)
    inverse_rms = lax.rsqrt(jnp.mean(summed * summed, axis=1) + small_eps)
    normed = summed * inverse_rms[:, None] * gain_cols.astype(jnp.float32)
    peak_abs = jnp.max(jnp.abs(normed), axis=1) + small_eps
    coded_rows = (normed / peak_abs[:, None]).astype(jnp.bfloat16)
    dispatched = jnp.dot(
        own_pick.astype(jnp.bfloat16), coded_rows, preferred_element_type=jnp.float32
    ).astype(jnp.bfloat16)
    slot_scale = jnp.dot(own_pick, peak_abs, precision=lax.Precision.HIGHEST)
    return (
        dispatched.reshape(experts_local, CAP, D),
        slot_scale.reshape(experts_local, CAP),
        slot_gate.reshape(experts_local, CAP),
    )


def solution(mesh):
    in_specs = (
        P("groups", "kv"),
        P("groups", "kv", None),
        P("groups"),
        P("kv", None),
        P("kv", None),
        P("groups", "kv"),
        P("kv"),
        P("groups", None),
        P("groups", None),
    )
    out_specs = (
        P(("groups", "kv"), None, None),
        P(("groups", "kv"), None),
        P(("groups", "kv"), None),
    )
    return jax.shard_map(
        per_device, mesh=mesh, in_specs=in_specs, out_specs=out_specs, check_vma=False
    )
```

profile of v0, /device:TPU:0, one launch (start us, length us, event | category | flops | bytes accessed | tf_op | source)
XLA Modules:
  0.0 314.2 jit_solution(11004834008479304627)
XLA Ops:
  7.2 0.0 copy-start
  7.2 0.0 all-gather.3.cloned.1.call-start
  7.2 0.7 all-gather.3.cloned.1.call-update
  7.9 0.0 reduce-scatter.2.cloned.1.call-start
  8.0 0.7 broadcast_compare_fusion.1
  8.7 43.6 %all-gather.3.cloned.1.call-done = bf16[40,18432]{1,0:T(8,128)(2,1)} async-done(((bf16[40,1152]{1,0:T(8,128)(2,1)}), bf16[40,18432]{1,0:T(8,128)(2,1)}) %all-gather.3.cloned.1.call-update) | async-done | bytes 1474576 | tf_op jit(solution)/shard_map/all_gather | solution.py:58
  52.3 3.3 %reshape.111 = bf16[40,32,576]{2,1,0:T(8,128)(2,1)S(1)} reshape(bf16[40,18432]{1,0:T(8,128)(2,1)} %all-gather.3.cloned.1.call-done) | data formatting | bytes 2949120 | tf_op jit(solution)/shard_map/reshape | solution.py:58
  55.5 3.9 %fusion.26 = (f32[40,32]{1,0:T(8,128)S(1)}, f32[40,32,128]{2,1,0:T(8,128)S(1)}) fusion(bf16[40,32,576]{2,1,0:T(8,128)(2,1)S(1)} %reshape.111, bf16[40,128,576]{1,2,0:T(8,128)(2,1)} %param.10, pred[40,128]{1,0:T(8,128)(4,1)S(1)} %broadcast_compare_fusion.1), kind=kOutput, calls=%fused_computation.47 | convolution fusion | flops 189233920 | bytes 8038400 | tf_op jit(solution)/shard_map/shq,scq->shc/dot_general | solution.py:61
  59.4 59.5 %pmax.7 = f32[40,32]{1,0:T(8,128)S(1)} all-reduce(f32[40,32]{1,0:T(8,128)S(1)} %get-tuple-element.5), channel_id=1, replica_groups=mesh['groups'=2,'kv'=16] {'kv'}, use_global_device_ids=true, to_apply=%region_3.4 | all-reduce | flops 1280 | bytes 10240 | tf_op jit(solution)/shard_map/pmax | solution.py:81
  118.9 0.4 fusion.7
  119.4 3.9 %fusion.2 = f32[40,32,512]{2,1,0:T(8,128)S(1)} fusion(bf16[40,128,576]{1,2,0:T(8,128)(2,1)} %param.10, f32[40,32]{1,0:T(8,128)S(1)} %get-tuple-element.4, f32[40,32,128]{2,1,0:T(8,128)S(1)} %get-tuple-element.6, f32[40,32]{1,0:T(8,128)S(1)} %get-tuple-element.5, pred[40,128]{1,0:T(8,128)(4,1)S(1)} %broadcast_compare_fusion.1), kind=kOutput, calls=%fused_computation.3 | convolution fusion | flops 168919040 | bytes 8535040 | tf_op jit(solution)/shard_map/shc,scl->shl/dot_general | solution.py:70
  123.3 3.0 copy.51
  126.3 0.0 copy-start.3
  126.3 0.0 copy-start.2
  126.3 0.0 reduce-scatter.2.cloned.1.call-update
  126.3 0.0 all-reduce.3.cloned.1.call-start
  126.4 0.6 copy-done.3
  127.0 0.1 copy.38
  127.1 0.1 eq.41
  127.2 0.2 convert_reduce_fusion
  127.4 0.1 reduce_sum.39
  127.5 0.1 copy.39
  127.6 0.0 copy-done.2
  127.6 19.1 %all-gather = bf16[16,448,40]{1,2,0:T(8,128)(2,1)S(1)} all-gather(bf16[1,448,40]{1,2,0:T(8,128)(2,1)S(1)} %bitcast.43), channel_id=1, replica_groups=mesh['groups'=2,'kv'=16] {'kv'}, dimensions={0}, use_global_device_ids=true | all-gather | bytes 609280 | tf_op jit(solution)/shard_map/all_gather | solution.py:109
  146.7 59.9 %psum.14 = f32[40,32]{1,0:T(8,128)S(1)} all-reduce(f32[40,32]{1,0:T(8,128)S(1)} %get-tuple-element.3), channel_id=1, replica_groups=mesh['groups'=2,'kv'=16] {'kv'}, use_global_device_ids=true, to_apply=%region_6.7 | all-reduce | flops 1280 | bytes 10240 | tf_op jit(solution)/shard_map/psum | solution.py:83
  206.7 0.1 constant_dynamic-slice_fusion
  206.7 0.0 reduce-scatter.2.cloned.1.call-done
  206.7 1.1 reshape.113
  207.8 0.1 broadcast_divide_fusion
  207.9 0.0 copy-done
  207.9 0.2 fusion.6
  208.2 3.8 %fusion.17 = f32[40,7168]{1,0:T(8,128)} fusion(bf16[256,7168]{1,0:T(8,128)(2,1)} %param.13, bf16[2,5,8,128]{3,2,1,0:T(8,128)(2,1)S(1)} %fusion.6), kind=kOutput, calls=%fused_computation.28 | convolution fusion | flops 146800640 | bytes 4837376 | tf_op jit(solution)/shard_map/dot_general | solution.py:100
  212.0 0.0 all-reduce.3.cloned.1.call-update
  212.1 0.2 copy.43
  212.3 0.0 copy-start.6
  212.3 0.0 copy-start.5
  212.3 0.0 copy-start.4
  212.3 0.5 reshape.125
  212.9 0.1 copy-done.6
  212.9 0.6 dynamic-slice
  214.2 0.0 copy-done.5
  214.2 0.3 dynamic-update-slice
  214.4 57.8 %all-reduce = bf16[7168]{0:T(1024)(128)(2,1)S(1)} all-reduce(bf16[7168]{0:T(1024)(128)(2,1)S(1)} %dynamic-update-slice), channel_id=1, replica_groups=mesh['groups'=2,'kv'=16] {'kv'}, use_global_device_ids=true, to_apply=%add | all-reduce | flops 7168 | bytes 28672
  272.3 0.0 copy-done.4
  272.3 0.1 copy.44
  272.3 0.1 reshape.128
  272.4 0.1 convert_reduce_fusion.1
  272.6 0.1 broadcast_compare_fusion
  272.7 0.8 fusion.15
  273.5 30.1 %all-reduce.3.cloned.1.call-done = f32[40,7168]{1,0:T(8,128)} async-done(((f32[40,7168]{1,0:T(8,128)}), f32[40,7168]{1,0:T(8,128)}) %all-reduce.3.cloned.1.call-update) | async-done | bytes 1146896 | tf_op jit(solution)/shard_map/psum | solution.py:107
  303.6 0.0 copy-start.1
  303.6 1.6 multiply_reduce_fusion
  305.1 0.0 copy-done.1
  305.2 0.4 abs_reduce_fusion
  305.5 0.4 convolution_convert_fusion
  306.0 0.9 reshape.116
  306.9 0.8 fusion.20
  (10 shorter events, 0.1 us)
Async XLA Ops:
  7.2 200.8 %copy-start = (bf16[1024,128]{1,0:T(8,128)(2,1)S(1)}, bf16[1024,128]{1,0:T(8,128)(2,1)}, u32[]{:S(2)}) copy-start(bf16[1024,128]{1,0:T(8,128)(2,1)} %param.12) | copy-start | bytes 786436
  7.2 45.1 %all-gather.3.cloned.1.call-start = ((), (), s32[]{:S(2)}) async-start(), calls=%async_computation.1 | async-start | bytes 1566720 | tf_op jit(solution)/shard_map/all_gather | solution.py:58
  7.9 198.8 %reduce-scatter.2.cloned.1.call-start = ((), (), s32[]{:S(2)}) async-start(), calls=%async_computation.2 | async-start | bytes 2785280 | tf_op jit(solution)/shard_map/reduce_scatter | solution.py:85
  126.3 0.7 copy-start.3
  126.3 1.3 copy-start.2
  126.3 177.2 %all-reduce.3.cloned.1.call-start = ((), (), s32[]{:S(2)}) async-start(), calls=%async_computation.3 | async-start | bytes 2293760 | tf_op jit(solution)/shard_map/psum | solution.py:107
  212.3 0.7 copy-start.6
  212.3 1.9 copy-start.5
  212.3 60.0 %copy-start.4 = (f32[40,8]{0,1:T(8,128)S(1)}, f32[40,8]{0,1:T(8,128)}, u32[]{:S(2)}) copy-start(f32[40,8]{0,1:T(8,128)} %param.17) | copy-start | bytes 3844
  303.6 1.6 copy-start.1
Sparse Core Ops, SparseCore 0:
  10.2 42.0 all-gather.2
  126.5 61.4 reduce-scatter.1
  212.2 91.3 all-reduce.2
where the time goes:
time: 315 us; the launch traced here: 314 us
  blocking collectives  196 us (62%)
  waiting for transfers between devices  74.4 us (24%)
  between operations  14.6 us (5%)
  matrix products  13.9 us (4%)
  local copies, waits for them, and re-layouts  11.1 us (4%)
  other arithmetic  3.74 us (1%)
    psum x1, blocking collectives, per_device(): weight_total = lax.psum(local_total * scaling, 'kv')  59.9 us
    pmax x1, blocking collectives, per_device(): global_max = lax.pmax(local_max, 'kv')  59.5 us
    unnamed x1, blocking collectives  57.8 us
    all_gather x1, waiting for transfers between devices, per_device(): lax.all_gather(queries, 'kv', axis=1, tiled=True)  43.6 us
    psum x1, waiting for transfers between devices, per_device(): attn_rows = lax.psum(partial_out, 'kv')  30.1 us
    all_gather x1, blocking collectives, per_device(): lax.all_gather(residual, 'kv', axis=1, tiled=True)  19.1 us
  transfers between devices with their start and end apart: 3, of which 2 were waited for; matrix products, arithmetic and copies ran while one was open for 1% of the time, Pallas kernels for 0%

commit v1 on v0

--- a/solution.py
+++ b/solution.py
@@ -104,7 +104,11 @@
     own_match = slot_match(targets, shard_index * slot_count, slot_count)
     own_pick = token_picker(own_match, seq_count)
     slot_gate = jnp.dot(own_match, gate_weights.reshape(-1), precision=lax.Precision.HIGHEST)
-    attn_rows = lax.psum(partial_out, "kv")
+    attn_rows = partial_out
+    for hop in (1, 2, 4, 8):
+        attn_rows = attn_rows + lax.ppermute(
+            attn_rows, "kv", [(dev, dev ^ hop) for dev in range(16)]
+        )
     resid_rows, gain_cols = (
         lax.all_gather(residual, "kv", axis=1, tiled=True),
         lax.all_gather(norm_gain, "kv", axis=0, tiled=True),

time: 315 us -> 369 us (1.17)
  blocking collectives: 196 us -> 245 us
    psum x1 -> x0, waiting for transfers between devices: 30.1 us -> none  [per_device(): attn_rows = lax.psum(partial_out, 'kv')]
    ppermute x0 -> x4, waiting for transfers between devices: none -> 29.1 us  [per_device(): lax.ppermute(attn_rows, 'kv', [(dev, dev ^ hop) for dev in range(16)])]
    unnamed x1, blocking collectives: 57.8 us -> 86.5 us
    all_gather x1, blocking collectives: 19.1 us -> 41.2 us  [per_device(): lax.all_gather(residual, 'kv', axis=1, tiled=True)]
  transfers between devices with their start and end apart: 3 -> 6, of which waited for: 2 -> 4; matrix products, arithmetic and copies ran while one was open for 1% -> 1% of each run, Pallas kernels for 0% -> 0%
where the time goes in v1:
time: 369 us; the launch traced here: 368 us
  blocking collectives  245 us (66%)
  waiting for transfers between devices  76.8 us (21%)
  between operations  14.9 us (4%)
  matrix products  12.8 us (3%)
  local copies, waits for them, and re-layouts  10.5 us (3%)
  other arithmetic  5.31 us (1%)
    unnamed x1, blocking collectives  86.5 us
    pmax x1, blocking collectives, per_device(): global_max = lax.pmax(local_max, 'kv')  59.5 us
    psum x1, blocking collectives, per_device(): weight_total = lax.psum(local_total * scaling, 'kv')  58.2 us
    all_gather x1, waiting for transfers between devices, per_device(): lax.all_gather(queries, 'kv', axis=1, tiled=True)  43.6 us
    all_gather x1, blocking collectives, per_device(): lax.all_gather(residual, 'kv', axis=1, tiled=True)  41.2 us
    ppermute x4, waiting for transfers between devices, per_device(): lax.ppermute(attn_rows, 'kv', [(dev, dev ^ hop) for dev in range(16)])  29.1 us
  transfers between devices with their start and end apart: 6, of which 4 were waited for; matrix products, arithmetic and copies ran while one was open for 1% of the time, Pallas kernels for 0%

profile of v1, /device:TPU:0, one launch (start us, length us, event | category | flops | bytes accessed | tf_op | source)
XLA Modules:
  0.0 368.2 jit_solution(16339214425957454617)
XLA Ops:
  7.2 0.0 copy-start
  7.2 0.0 all-gather.3.cloned.1.call-start
  7.2 0.7 all-gather.3.cloned.1.call-update
  7.9 0.0 reduce-scatter.2.cloned.1.call-start
  8.0 0.7 broadcast_compare_fusion.1
  8.7 43.6 %all-gather.3.cloned.1.call-done = bf16[40,18432]{1,0:T(8,128)(2,1)} async-done(((bf16[40,1152]{1,0:T(8,128)(2,1)}), bf16[40,18432]{1,0:T(8,128)(2,1)}) %all-gather.3.cloned.1.call-update) | async-done | bytes 1474576 | tf_op jit(solution)/shard_map/all_gather | solution.py:58
  52.3 3.3 reshape.111
  55.5 3.9 %fusion.26 = (f32[40,32]{1,0:T(8,128)S(1)}, f32[40,32,128]{2,1,0:T(8,128)S(1)}) fusion(bf16[40,32,576]{2,1,0:T(8,128)(2,1)S(1)} %reshape.111, bf16[40,128,576]{1,2,0:T(8,128)(2,1)} %param.10, pred[40,128]{1,0:T(8,128)(4,1)S(1)} %broadcast_compare_fusion.1), kind=kOutput, calls=%fused_computation.47 | convolution fusion | flops 189233920 | bytes 8038400 | tf_op jit(solution)/shard_map/shq,scq->shc/dot_general | solution.py:61
  59.4 59.5 %pmax.7 = f32[40,32]{1,0:T(8,128)S(1)} all-reduce(f32[40,32]{1,0:T(8,128)S(1)} %get-tuple-element.7), channel_id=1, replica_groups=mesh['groups'=2,'kv'=16] {'kv'}, use_global_device_ids=true, to_apply=%region_3.4 | all-reduce | flops 1280 | bytes 10240 | tf_op jit(solution)/shard_map/pmax | solution.py:81
  118.9 0.4 fusion.7
  119.4 3.9 %fusion.2 = f32[40,32,512]{2,1,0:T(8,128)S(1)} fusion(bf16[40,128,576]{1,2,0:T(8,128)(2,1)} %param.10, f32[40,32]{1,0:T(8,128)S(1)} %get-tuple-element.6, f32[40,32,128]{2,1,0:T(8,128)S(1)} %get-tuple-element.8, f32[40,32]{1,0:T(8,128)S(1)} %get-tuple-element.7, pred[40,128]{1,0:T(8,128)(4,1)S(1)} %broadcast_compare_fusion.1), kind=kOutput, calls=%fused_computation.3 | convolution fusion | flops 168919040 | bytes 8535040 | tf_op jit(solution)/shard_map/shc,scl->shl/dot_general | solution.py:70
  123.3 3.0 copy.51
  126.3 0.0 reduce-scatter.2.cloned.1.call-update
  126.3 58.2 %psum.7 = f32[40,32]{1,0:T(8,128)S(1)} all-reduce(f32[40,32]{1,0:T(8,128)S(1)} %get-tuple-element.5), channel_id=1, replica_groups=mesh['groups'=2,'kv'=16] {'kv'}, use_global_device_ids=true, to_apply=%region_6.7 | all-reduce | flops 1280 | bytes 10240 | tf_op jit(solution)/shard_map/psum | solution.py:83
  184.5 0.1 constant_dynamic-slice_fusion
  184.6 3.5 reduce-scatter.2.cloned.1.call-done
  188.1 1.1 reshape.113
  189.1 0.1 broadcast_divide_fusion
  189.3 0.0 copy-done
  189.3 0.2 fusion.6
  189.5 2.8 fusion.17
  192.3 0.1 collective-permute-start
  192.4 2.8 collective-permute-done
  195.1 0.1 add.79
  195.3 0.0 copy-start.2
  195.3 0.0 copy-start.1
  195.3 1.1 collective-permute-start.1
  196.4 26.3 %collective-permute-done.1 = f32[40,7168]{1,0:T(8,128)S(1)} collective-permute-done((f32[40,7168]{1,0:T(8,128)S(1)}, f32[40,7168]{1,0:T(8,128)S(1)}, u32[]{:S(2)}, u32[]{:S(2)}) %collective-permute-start.1) | collective-permute-done | bytes 1146912 | tf_op jit(solution)/shard_map/ppermute | solution.py:109
  222.7 0.1 add.80
  222.8 1.3 collective-permute-start.2
  224.0 0.0 copy-done.2
  224.0 0.1 copy.38
  224.1 0.1 eq.41
  224.2 0.2 convert_reduce_fusion
  224.4 0.0 copy-done.1
  224.4 41.2 %all-gather = bf16[16,448,40]{1,2,0:T(8,128)(2,1)S(1)} all-gather(bf16[1,448,40]{1,2,0:T(8,128)(2,1)S(1)} %bitcast.37), channel_id=1, replica_groups=mesh['groups'=2,'kv'=16] {'kv'}, dimensions={0}, use_global_device_ids=true | all-gather | bytes 609280 | tf_op jit(solution)/shard_map/all_gather | solution.py:113
  265.6 0.0 collective-permute-done.2
  265.6 1.1 add.81
  266.7 0.0 collective-permute-start.3
  266.7 0.2 copy.43
  267.0 0.0 copy-start.5
  267.0 0.0 copy-start.4
  267.0 0.0 copy-start.3
  267.0 0.5 reshape.125
  267.5 0.1 copy-done.5
  267.6 0.6 dynamic-slice
  268.9 0.0 copy-done.4
  268.9 0.3 dynamic-update-slice
  269.1 86.5 %all-reduce = bf16[7168]{0:T(1024)(128)(2,1)S(1)} all-reduce(bf16[7168]{0:T(1024)(128)(2,1)S(1)} %dynamic-update-slice), channel_id=1, replica_groups=mesh['groups'=2,'kv'=16] {'kv'}, use_global_device_ids=true, to_apply=%add | all-reduce | flops 7168 | bytes 28672
  355.6 0.1 reduce_sum.39
  355.7 0.1 copy.39
  355.8 0.0 copy-done.3
  355.8 0.1 copy.44
  355.8 0.1 reshape.128
  356.0 0.1 convert_reduce_fusion.1
  356.1 0.1 broadcast_compare_fusion
  356.2 0.8 fusion.15
  357.0 0.0 collective-permute-done.3
  357.0 1.9 multiply_reduce_fusion
  358.9 0.3 abs_reduce_fusion
  359.2 0.4 convolution_convert_fusion
  359.6 0.9 reshape.116
  360.6 0.8 fusion.20
  (10 shorter events, 0.1 us)
Async XLA Ops:
  7.2 182.1 %copy-start = (bf16[1024,128]{1,0:T(8,128)(2,1)S(1)}, bf16[1024,128]{1,0:T(8,128)(2,1)}, u32[]{:S(2)}) copy-start(bf16[1024,128]{1,0:T(8,128)(2,1)} %param.12) | copy-start | bytes 786436
  7.2 45.1 %all-gather.3.cloned.1.call-start = ((), (), s32[]{:S(2)}) async-start(), calls=%async_computation.1 | async-start | bytes 1566720 | tf_op jit(solution)/shard_map/all_gather | solution.py:58
  7.9 180.2 %reduce-scatter.2.cloned.1.call-start = ((), (), s32[]{:S(2)}) async-start(), calls=%async_computation.2 | async-start | bytes 2785280 | tf_op jit(solution)/shard_map/reduce_scatter | solution.py:85
  192.3 2.9 collective-permute-start
  195.3 28.8 %copy-start.2 = (s32[40,8]{0,1:T(8,128)S(1)}, s32[40,8]{0,1:T(8,128)}, u32[]{:S(2)}) copy-start(s32[40,8]{0,1:T(8,128)} %param.16) | copy-start | bytes 3844
  195.3 29.2 %copy-start.1 = (bf16[40,448]{1,0:T(8,128)(2,1)S(1)}, bf16[40,448]{1,0:T(8,128)(2,1)}, u32[]{:S(2)}) copy-start(bf16[40,448]{1,0:T(8,128)(2,1)} %param.14) | copy-start | bytes 107524
  195.3 27.4 %collective-permute-start.1 = (f32[40,7168]{1,0:T(8,128)S(1)}, f32[40,7168]{1,0:T(8,128)S(1)}, u32[]{:S(2)}, u32[]{:S(2)}) collective-permute-start(f32[40,7168]{1,0:T(8,128)S(1)} %add.79), channel_id=1, source_target_pairs={{0,2},{1,3},{2,0},{3,1},{4,6},{5,7},{6,4},{7,5},{8,10},{9,11},{10,... | collective-permute-start | bytes 3440648 | tf_op jit(solution)/shard_map/ppermute | solution.py:109
  222.8 42.8 %collective-permute-start.2 = (f32[40,7168]{1,0:T(8,128)S(1)}, f32[40,7168]{1,0:T(8,128)S(1)}, u32[]{:S(2)}, u32[]{:S(2)}) collective-permute-start(f32[40,7168]{1,0:T(8,128)S(1)} %add.80), channel_id=1, source_target_pairs={{0,4},{1,5},{2,6},{3,7},{4,0},{5,1},{6,2},{7,3},{8,12},{9,13},{10,... | collective-permute-start | bytes 3440648 | tf_op jit(solution)/shard_map/ppermute | solution.py:109
  266.7 90.3 %collective-permute-start.3 = (f32[40,7168]{1,0:T(8,128)}, f32[40,7168]{1,0:T(8,128)}, u32[]{:S(2)}, u32[]{:S(2)}) collective-permute-start(f32[40,7168]{1,0:T(8,128)} %add.81), channel_id=1, source_target_pairs={{0,8},{1,9},{2,10},{3,11},{4,12},{5,13},{6,14},{7,15},{8,0},{9,1},... | collective-permute-start | bytes 3440648 | tf_op jit(solution)/shard_map/ppermute | solution.py:109
  267.0 0.7 copy-start.5
  267.0 1.9 copy-start.4
  267.0 88.8 %copy-start.3 = (f32[40,8]{0,1:T(8,128)S(1)}, f32[40,8]{0,1:T(8,128)}, u32[]{:S(2)}) copy-start(f32[40,8]{0,1:T(8,128)} %param.17) | copy-start | bytes 3844
Sparse Core Ops, SparseCore 0:
  10.2 42.0 all-gather.2
  126.5 61.5 reduce-scatter.1
